TPU v7x, 32 devices: a whole 2x2x4 slice. The times are simulated.
32 devices in a mesh: dp: 4 (over z), mp: 8 (over y, x, core).
Axes of the slice: x: 2, y: 2, z: 4, core: 2. Of those that a mesh axis runs over, the one named last changes fastest.
Arguments:
- patches: bfloat16 [588, 768], P(None, ('dp', 'mp')), may hold values from -6 to 6
- embed_weight: bfloat16 [588, 6144], P(None, 'mp'), may hold values from -0.25 to 0.25
- embed_bias: float32 [6144], P('mp'), may hold values from -2 to 6
- pos_embed: bfloat16 [256, 6144], P(None, 'mp'), may hold values from -3 to 3
- norm_gain: float32 [6144], P('mp'), may hold values from 0.25 to 1.75
- inner_weight: bfloat16 [6144, 24576], P('dp', 'mp'), may hold values from -0.078125 to 0.078125
- inner_bias: float32 [24576], P('mp'), may hold values from -3 to 3
- outer_weight: bfloat16 [24576, 6144], P('mp', 'dp'), may hold values from -0.0546875 to 0.0546875
- outer_bias: float32 [6144], P('mp'), may hold values from -3 to 3
Outputs:
- block_out: float32 [768, 6144], P('dp', 'mp')
All inputs are finite; a program needn't handle non-finite values.
Results may differ from a plain program's by a relative error of at most 0.006.
Values may be sent and summed in bfloat16 or wider, within the bound.
A program may use at most 192 MiB of HBM per device.

v0:
```python
import jax
import jax.numpy as jnp
from jax import lax
from jax.sharding import PartitionSpec as P

D = 6144
PATCHES = 256


norm_eps = 1e-06


def contract_first(left, right):
    return lax.dot_general(
        left, right, (((0,), (0,)), ((), ())), preferred_element_type=jnp.float32
    )


def per_device(
    patches,
    embed_weight,
    embed_bias,
    pos_embed,
    norm_gain,
    inner_weight,
    inner_bias,
    outer_weight,
    outer_bias,
):
    group_rows = patches.shape[1] * lax.axis_size("mp")
    first_row = lax.axis_index("dp") * group_rows
    positions = (first_row + jnp.arange(group_rows, dtype=jnp.int32)) % PATCHES
    selector = (positions[:, None] == jnp.arange(PATCHES, dtype=jnp.int32)[None, :]).astype(
        jnp.bfloat16
    )
    all_patches = lax.all_gather(patches, "mp", axis=1, tiled=True)
    product = contract_first(all_patches, embed_weight)
    residual = product + embed_bias[None, :]
    residual = residual + jnp.dot(selector, pos_embed, preferred_element_type=jnp.float32)
    row_total = lax.psum(jnp.sum(residual, axis=1), "mp")
    row_mean = row_total / D
    centred = residual - row_mean[:, None]
    row_var = lax.psum(jnp.sum(centred * centred, axis=1), "mp") / D
    normed = (centred * lax.rsqrt(row_var + norm_eps)[:, None] * norm_gain[None, :]).astype(
        jnp.bfloat16
    )
    normed_all = lax.all_gather(normed, "mp", axis=1, tiled=True)
    preact = jnp.dot(
        normed_all,
        lax.all_gather(inner_weight, "dp", axis=0, tiled=True),
        preferred_element_type=jnp.float32,
    )
    hidden = jax.nn.gelu(preact + inner_bias[None, :], approximate=False).astype(jnp.bfloat16)
    partials = jnp.dot(
        hidden,
        lax.all_gather(outer_weight, "dp", axis=1, tiled=True),
        preferred_element_type=jnp.float32,
    )
    mlp_out = lax.psum_scatter(
        partials.astype(jnp.bfloat16), "mp", scatter_dimension=1, tiled=True
    ).astype(jnp.float32)
    return residual + mlp_out + outer_bias[None, :]


def solution(mesh):
    placed = (
        P(None, ("dp", "mp")),
        P(None, "mp"),
        P("mp"),
        P(None, "mp"),
        P("mp"),
        P("dp", "mp"),
        P("mp"),
        P("mp", "dp"),
        P("mp"),
    )
    return jax.shard_map(
        per_device, mesh=mesh, in_specs=placed, out_specs=P("dp", "mp"), check_vma=False
    )
```

profile of v0, /device:TPU:2, one launch (start us, length us, event | category | flops | bytes accessed | tf_op | source)
XLA Modules:
  0.0 1422.1 jit_solution(15980034112922536519)
XLA Ops:
  6.5 0.0 copy-start
  6.5 0.0 copy-start.2
  6.5 0.0 all-gather.4.cloned.1.call-start
  6.6 9.4 all_gather.12
  16.0 0.0 copy-done
  16.0 1.1 convolution_add_fusion.1
  17.1 1.4 fusion.74
  18.5 11.0 psum.14
  29.5 0.2 multiply_reduce_fusion
  29.7 11.8 psum.15
  41.5 0.0 copy-done.2
  41.5 0.9 multiply_convert_fusion
  42.4 0.0 all-gather.4.cloned.1.call-update
  42.4 0.0 all-gather.6.cloned.1.call-start
  42.5 0.7 all-gather.6.cloned.1.call-update
  43.2 0.0 copy-start.4
  43.2 0.0 all-gather.8.cloned.1.call-start
  43.2 0.7 all-gather.8.cloned.1.call-update
  43.9 0.0 reduce-scatter.2.cloned.1.call-start
  44.0 29.9 %all-gather.4.cloned.1.call-done = bf16[192,6144]{1,0:T(8,128)(2,1)} async-done(((bf16[192,768]{1,0:T(8,128)(2,1)}), bf16[192,6144]{1,0:T(8,128)(2,1)}) %all-gather.4.cloned.1.call-update) | async-done | bytes 2359312 | tf_op jit(solution)/shard_map/all_gather | solution.py:47
  73.9 633.1 %all-gather.6.cloned.1.call-done = bf16[6144,3072]{1,0:T(8,128)(2,1)} async-done(((bf16[1536,3072]{1,0:T(8,128)(2,1)}), bf16[6144,3072]{1,0:T(8,128)(2,1)}) %all-gather.6.cloned.1.call-update) | async-done | bytes 37748752 | tf_op jit(solution)/shard_map/all_gather | solution.py:50
  706.9 631.6 %all-gather.8.cloned.1.call-done = bf16[3072,6144]{1,0:T(8,128)(2,1)} async-done(((bf16[3072,1536]{1,0:T(8,128)(2,1)}), bf16[3072,6144]{1,0:T(8,128)(2,1)}) %all-gather.8.cloned.1.call-update) | async-done | bytes 37748752 | tf_op jit(solution)/shard_map/all_gather | solution.py:56
  1338.5 0.0 copy-done.4
  1338.5 0.0 copy-start.1
  1338.5 34.1 %convolution_convert_fusion = bf16[192,6144]{1,0:T(8,128)(2,1)} fusion(bf16[3072,6144]{1,0:T(8,128)(2,1)} %all-gather.8.cloned.1.call-done, bf16[192,6144]{1,0:T(8,128)(2,1)} %all-gather.4.cloned.1.call-done, bf16[6144,3072]{1,0:T(8,128)(2,1)} %all-gather.6.cloned.1.call-done, f32[3072]{0:T(1024)S(1)} %copy-done.4), kind=kOutput, calls=%fused_computation | convolution fusion | flops 14535622656 | bytes 80228352 | tf_op jit(solution)/shard_map/dot_general | solution.py:54
  1372.6 0.0 copy-start.3
  1372.6 0.0 reduce-scatter.2.cloned.1.call-update
  1372.6 41.0 %reduce-scatter.2.cloned.1.call-done = bf16[192,768]{1,0:T(8,128)(2,1)} async-done(((bf16[192,6144]{1,0:T(8,128)(2,1)}), bf16[192,768]{1,0:T(8,128)(2,1)}) %reduce-scatter.2.cloned.1.call-update) | async-done | bytes 294928 | tf_op jit(solution)/shard_map/reduce_scatter | solution.py:59
  1413.7 0.0 copy-done.3
  1413.7 1.9 add_add_fusion
  1415.5 0.0 copy-done.1
  (3 shorter events, 0.0 us)
Async XLA Ops:
  6.5 9.5 copy-start
  6.5 35.0 %copy-start.2 = (f32[768]{0:T(1024)S(1)}, f32[768]{0:T(1024)}, u32[]{:S(2)}) copy-start(f32[768]{0:T(1024)} %param.13) | copy-start | bytes 9220
  6.5 67.3 %all-gather.4.cloned.1.call-start = ((), (), s32[]{:S(2)}) async-start(), calls=%async_computation.1 | async-start | bytes 2654208 | tf_op jit(solution)/shard_map/all_gather | solution.py:47
  42.4 664.5 %all-gather.6.cloned.1.call-start = ((), (), s32[]{:S(2)}) async-start(), calls=%async_computation.2 | async-start | bytes 47185920 | tf_op jit(solution)/shard_map/all_gather | solution.py:50
  43.2 1295.4 %copy-start.4 = (f32[3072]{0:T(1024)S(1)}, f32[3072]{0:T(1024)}, u32[]{:S(2)}) copy-start(f32[3072]{0:T(1024)} %param.15) | copy-start | bytes 36868
  43.2 1295.3 %all-gather.8.cloned.1.call-start = ((), (), s32[]{:S(2)}) async-start(), calls=%async_computation.3 | async-start | bytes 47185920 | tf_op jit(solution)/shard_map/all_gather | solution.py:56
  43.9 1369.7 %reduce-scatter.2.cloned.1.call-start = ((), (), s32[]{:S(2)}) async-start(), calls=%async_computation.4 | async-start | bytes 2654208 | tf_op jit(solution)/shard_map/reduce_scatter | solution.py:59
  1338.5 77.0 %copy-start.1 = (bf16[588,768]{1,0:T(8,128)(2,1)S(1)}, bf16[588,768]{1,0:T(8,128)(2,1)}, u32[]{:S(2)}) copy-start(bf16[588,768]{1,0:T(8,128)(2,1)} %param.10) | copy-start | bytes 2709508
  1372.6 41.1 %copy-start.3 = (f32[768]{0:T(1024)S(1)}, f32[768]{0:T(1024)}, u32[]{:S(2)}) copy-start(f32[768]{0:T(1024)} %param.17) | copy-start | bytes 9220
Sparse Core Ops, SparseCore 0:
  42.6 31.2 all-gather.3
  75.5 631.4 all-gather.5
  708.5 629.9 all-gather.7
  1372.8 40.8 reduce-scatter.1
where the time goes:
time: 1420 us
  waiting for transfers between devices  1340 us (94%)
  matrix products  36.5 us (3%)
  blocking collectives  32.3 us (2%)
    all_gather x1, waiting for transfers between devices, per_device(): lax.all_gather(inner_weight, 'dp', axis=0, tiled=True)  633 us
    all_gather x1, waiting for transfers between devices, per_device(): lax.all_gather(outer_weight, 'dp', axis=1, tiled=True)  632 us
    reduce_scatter x1, waiting for transfers between devices, per_device(): lax.psum_scatter(partials.astype(jnp.bfloat16), 'mp', scatter_dimension=1...  41 us
    dot_general x1, matrix products, per_device(): jnp.dot(hidden, lax.all_gather(outer_weight, 'dp', axis=1, tiled=True), p...  34.1 us
    all_gather x1, waiting for transfers between devices, per_device(): normed_all = lax.all_gather(normed, 'mp', axis=1, tiled=True)  29.9 us
  transfers between devices with their start and end apart: 4, of which 4 were waited for; matrix products, arithmetic and copies ran while one was open for 0% of the time, Pallas kernels for 0%

commit v1 on v0

v1 whole, which is shorter than its diff:
```python
import jax
import jax.numpy as jnp
from jax import lax
from jax.sharding import PartitionSpec as P

norm_eps = 1e-06


def contract_first(left, right):
    return lax.dot_general(
        left, right, (((0,), (0,)), ((), ())), preferred_element_type=jnp.float32
    )


def per_device(
    patches,
    embed_weight,
    embed_bias,
    pos_embed,
    norm_gain,
    inner_weight,
    inner_bias,
    outer_weight,
    outer_bias,
):
    n_dp = lax.axis_size("dp")
    n_mp = lax.axis_size("mp")
    ratio = n_mp // n_dp
    group_rows = patches.shape[1] * n_mp
    width = embed_weight.shape[1]
    model_width = width * n_mp
    n_positions = pos_embed.shape[0]
    first_row = lax.axis_index("dp") * group_rows
    positions = (first_row + jnp.arange(group_rows, dtype=jnp.int32)) % n_positions
    selector = (positions[:, None] == jnp.arange(n_positions, dtype=jnp.int32)[None, :]).astype(
        jnp.bfloat16
    )
    all_patches = lax.all_gather(patches, "mp", axis=1, tiled=True)
    product = contract_first(all_patches, embed_weight)
    residual = product + embed_bias[None, :]
    residual = residual + jnp.dot(selector, pos_embed, preferred_element_type=jnp.float32)
    row_total = lax.psum(jnp.sum(residual, axis=1), "mp")
    row_mean = row_total / model_width
    centred = residual - row_mean[:, None]
    row_var = lax.psum(jnp.sum(centred * centred, axis=1), "mp") / model_width
    normed = (centred * lax.rsqrt(row_var + norm_eps)[:, None] * norm_gain[None, :]).astype(
        jnp.bfloat16
    )

    there = []
    for r in range(n_dp):
        for c in range(n_mp):
            there.append((r * n_mp + c, (c // ratio) * n_mp + r * ratio + c % ratio))
    back = [(b, a) for a, b in there]
    moved = lax.ppermute(normed, ("dp", "mp"), there)
    blocks = lax.all_gather(moved, "mp", axis=0, tiled=False)
    own_rows = (
        blocks.reshape(n_dp, ratio, group_rows, width)
        .transpose(0, 2, 1, 3)
        .reshape(n_dp * group_rows, ratio * width)
    )
    preact_part = jnp.dot(own_rows, inner_weight, preferred_element_type=jnp.float32)
    preact = lax.psum_scatter(
        preact_part.astype(jnp.bfloat16), "dp", scatter_dimension=0, tiled=True
    ).astype(jnp.float32)
    hidden = jax.nn.gelu(preact + inner_bias[None, :], approximate=False).astype(jnp.bfloat16)
    all_hidden = lax.all_gather(hidden, "dp", axis=0, tiled=True)
    partials = jnp.dot(all_hidden, outer_weight, preferred_element_type=jnp.float32).astype(
        jnp.bfloat16
    )
    partials = (
        partials.reshape(n_dp, group_rows, ratio, width)
        .transpose(0, 2, 1, 3)
        .reshape(n_mp * group_rows, width)
    )
    summed = lax.psum_scatter(partials, "mp", scatter_dimension=0, tiled=True)
    mlp_out = lax.ppermute(summed, ("dp", "mp"), back).astype(jnp.float32)
    return residual + mlp_out + outer_bias[None, :]


def solution(mesh):
    placed = (
        P(None, ("dp", "mp")),
        P(None, "mp"),
        P("mp"),
        P(None, "mp"),
        P("mp"),
        P("dp", "mp"),
        P("mp"),
        P("mp", "dp"),
        P("mp"),
    )
    return jax.shard_map(
        per_device, mesh=mesh, in_specs=placed, out_specs=P("dp", "mp"), check_vma=False
    )
```

time: 1420 us -> 386 us (0.27)
  waiting for transfers between devices: 1340 us -> 286 us
    all_gather x3 -> x2, waiting for transfers between devices: 1290 us -> 119 us  [the longest x1 89.8 us: per_device(): all_hidden = lax.all_gather(hidden, 'dp', axis=0, tiled=True)]
    reduce_scatter x1 -> x2, waiting for transfers between devices: 41 us -> 126 us  [the longest x1 85.4 us: per_device(): lax.psum_scatter(preact_part.astype(jnp.bfloat16), 'dp', scatter_dimensio...]
    ppermute x0 -> x2, waiting for transfers between devices: none -> 40.5 us  [the longest x1 20.8 us: per_device(): mlp_out = lax.ppermute(summed, ('dp', 'mp'), back).astype(jnp.float32)]
    dot_general x1 -> x2, matrix products: 34.1 us -> 21.6 us  [the longest x1 12.5 us: per_device(): jnp.dot(all_hidden, outer_weight, preferred_element_type=jnp.float32)]
  transfers between devices with their start and end apart: 4 -> 6, of which waited for: 4 -> 6; matrix products, arithmetic and copies ran while one was open for 0% -> 0% of each run, Pallas kernels for 0% -> 0%
where the time goes in v1:
time: 386 us
  waiting for transfers between devices  286 us (74%)
  blocking collectives  32.3 us (8%)
  matrix products  24.1 us (6%)
  between operations  13.2 us (3%)
  local copies, waits for them, and re-layouts  12.1 us (3%)
  starting transfers between devices  9.52 us (2%)
  other arithmetic  8.31 us (2%)
    all_gather x1, waiting for transfers between devices, per_device(): all_hidden = lax.all_gather(hidden, 'dp', axis=0, tiled=True)  89.8 us
    reduce_scatter x1, waiting for transfers between devices, per_device(): lax.psum_scatter(preact_part.astype(jnp.bfloat16), 'dp', scatter_dimensio...  85.4 us
    reduce_scatter x1, waiting for transfers between devices, per_device(): summed = lax.psum_scatter(partials, 'mp', scatter_dimension=0, tiled=True)  40.9 us
    all_gather x1, waiting for transfers between devices, per_device(): blocks = lax.all_gather(moved, 'mp', axis=0, tiled=False)  29.6 us
    ppermute x1, waiting for transfers between devices, per_device(): mlp_out = lax.ppermute(summed, ('dp', 'mp'), back).astype(jnp.float32)  20.8 us
    ppermute x1, waiting for transfers between devices, per_device(): moved = lax.ppermute(normed, ('dp', 'mp'), there)  19.7 us
    dot_general x1, matrix products, per_device(): jnp.dot(all_hidden, outer_weight, preferred_element_type=jnp.float32)  12.5 us
    psum x1, blocking collectives, per_device(): row_var = lax.psum(jnp.sum(centred * centred, axis=1), 'mp') / model_width  11.8 us
  transfers between devices with their start and end apart: 6, of which 6 were waited for; matrix products, arithmetic and copies ran while one was open for 0% of the time, Pallas kernels for 0%

profile of v1, /device:TPU:2, one launch (start us, length us, event | category | flops | bytes accessed | tf_op | source)
XLA Modules:
  0.0 385.8 jit_solution(2165305708302340001)
XLA Ops:
  6.5 0.0 copy-start
  6.5 0.0 copy-start.5
  6.5 0.0 all-gather.6.cloned.1.call-start
  6.6 9.4 %all_gather.12 = bf16[588,192]{0,1:T(8,128)(2,1)S(1)} all-gather(bf16[588,24]{0,1:T(8,128)(2,1)} %param.9), channel_id=1, replica_groups=mesh['dp'=4,'mp'=8] {'mp'}, dimensions={1}, use_global_device_ids=true | all-gather | bytes 254016 | tf_op jit(solution)/shard_map/all_gather | solution.py:38
  16.0 0.0 copy-done
  16.0 1.1 convolution_add_fusion
  17.1 1.4 fusion.15
  18.5 0.0 copy-start.1
  18.5 11.0 %psum.14 = f32[192]{0:T(256)S(1)} all-reduce(f32[192]{0:T(256)S(1)} %get-tuple-element.5), channel_id=1, replica_groups=mesh['dp'=4,'mp'=8] {'mp'}, use_global_device_ids=true, to_apply=%region_1.2 | all-reduce | flops 192 | bytes 1536 | tf_op jit(solution)/shard_map/psum | solution.py:42
  29.5 0.2 multiply_reduce_fusion
  29.7 11.8 %psum.15 = f32[192]{0:T(256)S(1)} all-reduce(f32[192]{0:T(256)S(1)} %multiply_reduce_fusion), channel_id=1, replica_groups=mesh['dp'=4,'mp'=8] {'mp'}, use_global_device_ids=true, to_apply=%region_3.4 | all-reduce | flops 192 | bytes 1536 | tf_op jit(solution)/shard_map/psum | solution.py:45
  41.6 0.0 copy-done.5
  41.6 0.2 multiply_convert_fusion
  41.7 5.8 %collective-permute-start = (bf16[192,768]{1,0:T(8,128)(2,1)S(1)}, bf16[192,768]{1,0:T(8,128)(2,1)S(1)}, u32[]{:S(2)}, u32[]{:S(2)}) collective-permute-start(bf16[192,768]{1,0:T(8,128)(2,1)S(1)} %multiply_convert_fusion), channel_id=1, source_target_pairs={{0,0},{1,1},{2,8},{3,9},{4,16},{5,17},{6,24},{7,25},{8,2},{9,3},{1... | collective-permute-start | bytes 884744 | tf_op jit(solution)/shard_map/ppermute | solution.py:55
  47.6 19.7 %collective-permute-done = bf16[192,768]{1,0:T(8,128)(2,1)S(1)} collective-permute-done((bf16[192,768]{1,0:T(8,128)(2,1)S(1)}, bf16[192,768]{1,0:T(8,128)(2,1)S(1)}, u32[]{:S(2)}, u32[]{:S(2)}) %collective-permute-start) | collective-permute-done | bytes 294944 | tf_op jit(solution)/shard_map/ppermute | solution.py:55
  67.2 0.0 copy-start.3
  67.2 0.7 copy-done.3
  67.9 0.0 all-gather.6.cloned.1.call-update
  68.0 0.0 reduce-scatter.3.cloned.1.call-start
  68.0 29.6 %all-gather.6.cloned.1.call-done = bf16[1536,768]{1,0:T(8,128)(2,1)} async-done(((bf16[192,768]{1,0:T(8,128)(2,1)}), bf16[1536,768]{1,0:T(8,128)(2,1)}) %all-gather.6.cloned.1.call-update) | async-done | bytes 2359312 | tf_op jit(solution)/shard_map/all_gather | solution.py:56
  97.6 0.0 copy-start.7
  97.6 4.2 %copy.11 = bf16[4,2,192,768]{3,1,2,0:T(2,128)(2,1)S(1)} copy(bf16[4,2,192,768]{3,2,1,0:T(8,128)(2,1)} %bitcast.17) | data formatting | bytes 4718592 | tf_op jit(solution)/shard_map/reshape | solution.py:58
  101.8 0.0 copy-done.1
  101.8 0.4 copy.13
  102.3 0.0 copy-done.7
  102.3 9.1 %convolution_convert_fusion = bf16[768,3072]{1,0:T(8,128)(2,1)} fusion(bf16[768,1536]{1,0:T(8,128)(2,1)S(1)} %bitcast.18, bf16[1536,3072]{1,0:T(8,128)(2,1)S(1)} %copy-done.7), kind=kOutput, calls=%fused_computation | convolution fusion | flops 7250116608 | bytes 16515072 | tf_op jit(solution)/shard_map/dot_general | solution.py:62
  111.4 0.0 copy-start.4
  111.4 0.0 reduce-scatter.3.cloned.1.call-update
  111.5 0.0 all-gather.4.cloned.1.call-start
  111.5 85.4 %reduce-scatter.3.cloned.1.call-done = bf16[192,3072]{1,0:T(8,128)(2,1)} async-done(((bf16[768,3072]{1,0:T(8,128)(2,1)}), bf16[192,3072]{1,0:T(8,128)(2,1)}) %reduce-scatter.3.cloned.1.call-update) | async-done | bytes 1179664 | tf_op jit(solution)/shard_map/reduce_scatter | solution.py:63
  196.9 0.0 copy-done.4
  196.9 7.0 %fusion.2 = bf16[192,3072]{1,0:T(8,128)(2,1)} fusion(bf16[192,3072]{1,0:T(8,128)(2,1)} %reduce-scatter.3.cloned.1.call-done, f32[3072]{0:T(1024)S(1)} %copy-done.4), kind=kLoop, calls=%fused_computation.5 | loop fusion | flops 39518208 | bytes 2371584 | tf_op jit(solution)/shard_map/convert_element_type | solution.py:66
  203.9 0.0 all-gather.4.cloned.1.call-update
  203.9 0.2 reduce-scatter.5.cloned.1.call-start
  204.2 89.8 %all-gather.4.cloned.1.call-done = bf16[768,3072]{1,0:T(8,128)(2,1)} async-done(((bf16[192,3072]{1,0:T(8,128)(2,1)}), bf16[768,3072]{1,0:T(8,128)(2,1)}) %all-gather.4.cloned.1.call-update) | async-done | bytes 4718608 | tf_op jit(solution)/shard_map/all_gather | solution.py:67
  294.0 12.5 %convolution_convert_fusion.1 = bf16[768,1536]{1,0:T(8,128)(2,1)} fusion(bf16[768,3072]{1,0:T(8,128)(2,1)} %all-gather.4.cloned.1.call-done, bf16[3072,1536]{1,0:T(8,128)(2,1)} %param.16), kind=kOutput, calls=%fused_computation.2 | convolution fusion | flops 7248936960 | bytes 16515072 | tf_op jit(solution)/shard_map/dot_general | solution.py:68
  306.5 5.0 %reshape.35 = bf16[4,192,2,768]{3,2,1,0:T(2,128)(2,1)S(1)} reshape(bf16[768,1536]{1,0:T(8,128)(2,1)} %convolution_convert_fusion.1) | data formatting | bytes 4718592 | tf_op jit(solution)/shard_map/reshape | solution.py:72
  311.5 1.7 copy.12
  313.2 0.0 copy-start.2
  313.2 0.0 copy-start.6
  313.2 0.0 reduce-scatter.5.cloned.1.call-update
  313.2 40.9 %reduce-scatter.5.cloned.1.call-done = bf16[192,768]{1,0:T(8,128)(2,1)} async-done(((bf16[1536,768]{1,0:T(8,128)(2,1)}), bf16[192,768]{1,0:T(8,128)(2,1)}) %reduce-scatter.5.cloned.1.call-update) | async-done | bytes 294928 | tf_op jit(solution)/shard_map/reduce_scatter | solution.py:76
  354.1 3.4 collective-permute-start.1
  357.5 20.8 %collective-permute-done.1 = bf16[192,768]{1,0:T(8,128)(2,1)S(1)} collective-permute-done((bf16[192,768]{1,0:T(8,128)(2,1)}, bf16[192,768]{1,0:T(8,128)(2,1)S(1)}, u32[]{:S(2)}, u32[]{:S(2)}) %collective-permute-start.1) | collective-permute-done | bytes 294944 | tf_op jit(solution)/shard_map/ppermute | solution.py:77
  378.3 0.0 copy-done.2
  378.3 0.0 copy-done.6
  378.3 0.9 add_add_fusion
  (3 shorter events, 0.0 us)
Async XLA Ops:
  6.5 9.5 %copy-start = (bf16[588,768]{1,0:T(8,128)(2,1)S(1)}, bf16[588,768]{1,0:T(8,128)(2,1)}, u32[]{:S(2)}) copy-start(bf16[588,768]{1,0:T(8,128)(2,1)} %param.10) | copy-start | bytes 2709508
  6.5 35.0 %copy-start.5 = (f32[768]{0:T(1024)S(1)}, f32[768]{0:T(1024)}, u32[]{:S(2)}) copy-start(f32[768]{0:T(1024)} %param.13) | copy-start | bytes 9220
  6.5 91.0 %all-gather.6.cloned.1.call-start = ((), (), s32[]{:S(2)}) async-start(), calls=%async_computation.5 | async-start | bytes 2654208 | tf_op jit(solution)/shard_map/all_gather | solution.py:56
  18.5 83.4 %copy-start.1 = (f32[192,768]{1,0:T(8,128)}, f32[192,768]{1,0:T(8,128)S(1)}, u32[]{:S(2)}) copy-start(f32[192,768]{1,0:T(8,128)S(1)} %get-tuple-element.6) | copy-start | bytes 1769476
  41.7 25.5 %collective-permute-start = (bf16[192,768]{1,0:T(8,128)(2,1)S(1)}, bf16[192,768]{1,0:T(8,128)(2,1)S(1)}, u32[]{:S(2)}, u32[]{:S(2)}) collective-permute-start(bf16[192,768]{1,0:T(8,128)(2,1)S(1)} %multiply_convert_fusion), channel_id=1, source_target_pairs={{0,0},{1,1},{2,8},{3,9},{4,16},{5,17},{6,24},{7,25},{8,2},{9,3},{1... | collective-permute-start | bytes 884744 | tf_op jit(solution)/shard_map/ppermute | solution.py:55
  67.2 0.7 copy-start.3
  68.0 128.9 %reduce-scatter.3.cloned.1.call-start = ((), (), s32[]{:S(2)}) async-start(), calls=%async_computation.2 | async-start | bytes 5898240 | tf_op jit(solution)/shard_map/reduce_scatter | solution.py:63
  97.6 4.7 %copy-start.7 = (bf16[1536,3072]{1,0:T(8,128)(2,1)S(1)}, bf16[1536,3072]{1,0:T(8,128)(2,1)}, u32[]{:S(2)}) copy-start(bf16[1536,3072]{1,0:T(8,128)(2,1)} %param.14) | copy-start | bytes 28311556
  111.4 85.5 %copy-start.4 = (f32[3072]{0:T(1024)S(1)}, f32[3072]{0:T(1024)}, u32[]{:S(2)}) copy-start(f32[3072]{0:T(1024)} %param.15) | copy-start | bytes 36868
  111.5 182.6 %all-gather.4.cloned.1.call-start = ((), (), s32[]{:S(2)}) async-start(), calls=%async_computation.3 | async-start | bytes 5898240 | tf_op jit(solution)/shard_map/all_gather | solution.py:67
  203.9 150.2 %reduce-scatter.5.cloned.1.call-start = ((), (), s32[]{:S(2)}) async-start(), calls=%async_computation.4 | async-start | bytes 2654208 | tf_op jit(solution)/shard_map/reduce_scatter | solution.py:76
  313.2 65.2 %copy-start.2 = (f32[192,768]{1,0:T(8,128)S(1)}, f32[192,768]{1,0:T(8,128)}, u32[]{:S(2)}) copy-start(f32[192,768]{1,0:T(8,128)} %copy-done.1) | copy-start | bytes 1769476
  313.2 65.2 %copy-start.6 = (f32[768]{0:T(1024)S(1)}, f32[768]{0:T(1024)}, u32[]{:S(2)}) copy-start(f32[768]{0:T(1024)} %param.17) | copy-start | bytes 9220
  354.1 24.2 %collective-permute-start.1 = (bf16[192,768]{1,0:T(8,128)(2,1)}, bf16[192,768]{1,0:T(8,128)(2,1)S(1)}, u32[]{:S(2)}, u32[]{:S(2)}) collective-permute-start(bf16[192,768]{1,0:T(8,128)(2,1)} %reduce-scatter.5.cloned.1.call-done), channel_id=1, source_target_pairs={{0,0},{1,1},{8,2},{9,3},{16,4},{17,5},{24,6},{25,7},{2,8},{3,9},{1... | collective-permute-start | bytes 884744 | tf_op jit(solution)/shard_map/ppermute | solution.py:77
Sparse Core Ops, SparseCore 0:
  68.1 29.4 all-gather.5
  111.6 85.2 reduce-scatter.2
  204.1 89.9 all-gather.3
  313.3 40.7 reduce-scatter.4

commit v2 on v1

--- a/solution.py
+++ b/solution.py
@@ -1,6 +1,10 @@
+import functools
+
 import jax
 import jax.numpy as jnp
 from jax import lax
+from jax.experimental import pallas as pl
+from jax.experimental.pallas import tpu as pltpu
 from jax.sharding import PartitionSpec as P
 
 norm_eps = 1e-06
@@ -10,6 +14,172 @@
     return lax.dot_general(
         left, right, (((0,), (0,)), ((), ())), preferred_element_type=jnp.float32
     )
+
+LANES = 128
+
+
+def line_kernel(n, part, bias, out, from_left, from_right, send_sems, left_sems, right_sems, block_sems):
+    z = lax.axis_index("dp")
+    total, columns = part.shape
+    rows = total // n
+    chunks = columns // LANES
+    settled = [max(k, n - 1 - k) for k in range(n)]
+    steps = chunks + max(settled[o] + abs(k - o) for o in range(n) for k in range(n))
+
+    def at(ref, first, last, c):
+        lanes = pl.ds(pl.multiple_of(c * LANES, LANES), LANES)
+        return ref.at[pl.ds(first * rows, (last - first) * rows), lanes]
+
+    def send(src, dst, send_sem, recv_sem, to):
+        return pltpu.make_async_remote_copy(
+            src_ref=src,
+            dst_ref=dst,
+            send_sem=send_sem,
+            recv_sem=recv_sem,
+            device_id={"dp": to},
+            device_id_type=pl.DeviceIdType.MESH,
+        )
+
+    barrier = pltpu.get_barrier_semaphore()
+    for k in range(n):
+
+        @pl.when(z == k)
+        def _(k=k):
+            near = [o for o in (k - 1, k + 1) if 0 <= o < n]
+            for o in near:
+                pl.semaphore_signal(
+                    barrier, inc=1, device_id={"dp": o}, device_id_type=pl.DeviceIdType.MESH
+                )
+            pl.semaphore_wait(barrier, len(near))
+
+    def role(k):
+        has_left, has_right = k > 0, k < n - 1
+
+        def wait_left(c):
+            at_c = at(from_left, k, n, c)
+            send(at_c, at_c, send_sems.at[0], left_sems.at[c], k - 1).wait_recv()
+
+        def wait_right(c):
+            at_c = at(from_right, 0, k + 1, c)
+            send(at_c, at_c, send_sems.at[1], right_sems.at[c], k + 1).wait_recv()
+
+        def add_own(ref, first, last, c):
+            held = at(ref, first, last, c)
+            own = at(part, first, last, c)
+            held[...] = (held[...].astype(jnp.float32) + own[...].astype(jnp.float32)).astype(
+                jnp.bfloat16
+            )
+
+        def pass_right(c):
+            src = part
+            if has_left:
+                wait_left(c)
+                add_own(from_left, k + 1, n, c)
+                src = from_left
+            send(
+                at(src, k + 1, n, c),
+                at(from_left, k + 1, n, c),
+                send_sems.at[0],
+                left_sems.at[c],
+                k + 1,
+            ).start()
+
+        def pass_left(c):
+            src = part
+            if has_right:
+                wait_right(c)
+                add_own(from_right, 0, k, c)
+                src = from_right
+            send(
+                at(src, 0, k, c),
+                at(from_right, 0, k, c),
+                send_sems.at[1],
+                right_sems.at[c],
+                k - 1,
+            ).start()
+
+        def give(c, origin, to):
+            block = at(out, origin, origin + 1, c)
+            sem = send_sems.at[2] if to > k else send_sems.at[3]
+            return send(block, block, sem, block_sems.at[origin, c], to)
+
+        def settle(c):
+            if not has_right:
+                wait_left(c)
+            if not has_left:
+                wait_right(c)
+            x = at(part, k, k + 1, c)[...].astype(jnp.float32)
+            if has_left:
+                x = x + at(from_left, k, k + 1, c)[...].astype(jnp.float32)
+            if has_right:
+                x = x + at(from_right, k, k + 1, c)[...].astype(jnp.float32)
+            x = x + bias[:, pl.ds(pl.multiple_of(c * LANES, LANES), LANES)]
+            x = 0.5 * x * (1.0 + lax.erf(x * (0.5**0.5)))
+            at(out, k, k + 1, c)[...] = x.astype(jnp.bfloat16)
+            if has_right:
+                give(c, k, k + 1).start()
+            if has_left:
+                give(c, k, k - 1).start()
+
+        def relay(origin, c):
+            give(c, origin, k - 1 if origin < k else k + 1).wait_recv()
+            to = k + 1 if origin < k else k - 1
+            if 0 <= to < n:
+                give(c, origin, to).start()
+
+        def run(c, action):
+            @pl.when(jnp.logical_and(c >= 0, c < chunks))
+            def _():
+                action(c)
+
+        def step(s, carry):
+            if has_right:
+                run(s - k, pass_right)
+            if has_left:
+                run(s - (n - 1 - k), pass_left)
+            run(s - settled[k], settle)
+            for origin in sorted((o for o in range(n) if o != k), key=lambda o: -abs(o - k)):
+                run(s - settled[origin] - abs(origin - k), functools.partial(relay, origin))
+            return carry
+
+        lax.fori_loop(0, steps, step, 0)
+
+        def drain(ref, first, last, sem, to):
+            sent = ref.at[pl.ds(first * rows, (last - first) * rows), :]
+            send(sent, sent, sem, block_sems.at[0, 0], to).wait_send()
+
+        if has_right:
+            drain(part, k + 1, n, send_sems.at[0], k + 1)
+            drain(out, 0, k + 1, send_sems.at[2], k + 1)
+        if has_left:
+            drain(part, 0, k, send_sems.at[1], k - 1)
+            drain(out, k, n, send_sems.at[3], k - 1)
+
+    for k in range(n):
+        pl.when(z == k)(functools.partial(role, k))
+
+
+def hidden_of(n, part, bias):
+    total, columns = part.shape
+    chunks = columns // LANES
+    vmem = pl.BlockSpec(memory_space=pltpu.VMEM)
+    return pl.pallas_call(
+        functools.partial(line_kernel, n),
+        out_shape=jax.ShapeDtypeStruct(part.shape, jnp.bfloat16),
+        in_specs=[vmem, vmem],
+        out_specs=vmem,
+        scratch_shapes=[
+            pltpu.VMEM(part.shape, jnp.bfloat16),
+            pltpu.VMEM(part.shape, jnp.bfloat16),
+            pltpu.SemaphoreType.DMA((4,)),
+            pltpu.SemaphoreType.DMA((chunks,)),
+            pltpu.SemaphoreType.DMA((chunks,)),
+            pltpu.SemaphoreType.DMA((n, chunks)),
+        ],
+        compiler_params=pltpu.CompilerParams(
+            collective_id=0, has_side_effects=True, vmem_limit_bytes=40 * 1024 * 1024
+        ),
+    )(part, bias)
 
 
 def per_device(
@@ -60,11 +230,7 @@
         .reshape(n_dp * group_rows, ratio * width)
     )
     preact_part = jnp.dot(own_rows, inner_weight, preferred_element_type=jnp.float32)
-    preact = lax.psum_scatter(
-        preact_part.astype(jnp.bfloat16), "dp", scatter_dimension=0, tiled=True
-    ).astype(jnp.float32)
-    hidden = jax.nn.gelu(preact + inner_bias[None, :], approximate=False).astype(jnp.bfloat16)
-    all_hidden = lax.all_gather(hidden, "dp", axis=0, tiled=True)
+    all_hidden = hidden_of(n_dp, preact_part.astype(jnp.bfloat16), inner_bias[None, :])
     partials = jnp.dot(all_hidden, outer_weight, preferred_element_type=jnp.float32).astype(
         jnp.bfloat16
     )

time: 386 us -> 322 us (0.83)
  waiting for transfers between devices: 286 us -> 112 us
  Pallas kernels: 0 us -> 121 us
  other arithmetic: 8.31 us -> 3.03 us
  matrix products: 24.1 us -> 18.9 us
    pallas_call x0 -> x1, Pallas kernels: none -> 121 us  [hidden_of(): pl.pallas_call(functools.partial(line_kernel, n), out_shape=jax.ShapeDtyp...]
    all_gather x1 -> x0, waiting for transfers between devices: 89.8 us -> none  [per_device(): all_hidden = lax.all_gather(hidden, 'dp', axis=0, tiled=True)]
    reduce_scatter x1 -> x0, waiting for transfers between devices: 85.4 us -> none  [per_device(): lax.psum_scatter(preact_part.astype(jnp.bfloat16), 'dp', scatter_dimensio...]
    convert_element_type x1 -> x0, other arithmetic: 7.03 us -> none  [per_device(): jax.nn.gelu(preact + inner_bias[None, :], approximate=False)]
  transfers between devices with their start and end apart: 6 -> 4, of which waited for: 6 -> 4; matrix products, arithmetic and copies ran while one was open for 0% -> 0% of each run, Pallas kernels for 0% -> 0%
where the time goes in v2:
time: 322 us
  Pallas kernels  121 us (38%)
  waiting for transfers between devices  112 us (35%)
  blocking collectives  32.3 us (10%)
  matrix products  18.9 us (6%)
  between operations  13.6 us (4%)
  local copies, waits for them, and re-layouts  12.1 us (4%)
  starting transfers between devices  9.25 us (3%)
    pallas_call x1, Pallas kernels, hidden_of(): pl.pallas_call(functools.partial(line_kernel, n), out_shape=jax.ShapeDtyp...  121 us
    reduce_scatter x1, waiting for transfers between devices, per_device(): summed = lax.psum_scatter(partials, 'mp', scatter_dimension=0, tiled=True)  42 us
    all_gather x1, waiting for transfers between devices, per_device(): blocks = lax.all_gather(moved, 'mp', axis=0, tiled=False)  29.6 us
    ppermute x1, waiting for transfers between devices, per_device(): mlp_out = lax.ppermute(summed, ('dp', 'mp'), back).astype(jnp.float32)  20.8 us
    ppermute x1, waiting for transfers between devices, per_device(): moved = lax.ppermute(normed, ('dp', 'mp'), there)  19.7 us
    psum x1, blocking collectives, per_device(): row_var = lax.psum(jnp.sum(centred * centred, axis=1), 'mp') / model_width  11.9 us
    psum x1, blocking collectives, per_device(): row_total = lax.psum(jnp.sum(residual, axis=1), 'mp')  11 us
    all_gather x1, blocking collectives, per_device(): all_patches = lax.all_gather(patches, 'mp', axis=1, tiled=True)  9.44 us
  transfers between devices with their start and end apart: 4, of which 4 were waited for; matrix products, arithmetic and copies ran while one was open for 0% of the time, Pallas kernels for 0%

profile of v2, /device:TPU:2, one launch (start us, length us, event | category | flops | bytes accessed | tf_op | source)
XLA Modules:
  0.0 321.8 jit_solution(12404516622143392486)
XLA Ops:
  6.5 0.0 copy-start
  6.5 0.0 all-gather.3.cloned.1.call-start
  6.6 9.4 %all_gather.9 = bf16[588,192]{0,1:T(8,128)(2,1)S(1)} all-gather(bf16[588,24]{0,1:T(8,128)(2,1)} %param.9), channel_id=1, replica_groups=mesh['dp'=4,'mp'=8] {'mp'}, dimensions={1}, use_global_device_ids=true | all-gather | bytes 254016 | tf_op jit(solution)/shard_map/all_gather | solution.py:208
  16.0 0.0 copy-done
  16.0 1.1 convolution_add_fusion
  17.1 1.4 fusion.2
  18.5 0.0 copy-start.2
  18.5 11.0 %psum.14 = f32[192]{0:T(256)S(1)} all-reduce(f32[192]{0:T(256)S(1)} %get-tuple-element.5), channel_id=1, replica_groups=mesh['dp'=4,'mp'=8] {'mp'}, use_global_device_ids=true, to_apply=%region_1.2 | all-reduce | flops 192 | bytes 1536 | tf_op jit(solution)/shard_map/psum | solution.py:212
  29.5 0.2 multiply_reduce_fusion
  29.7 11.9 %psum.15 = f32[192]{0:T(256)S(1)} all-reduce(f32[192]{0:T(256)S(1)} %multiply_reduce_fusion), channel_id=1, replica_groups=mesh['dp'=4,'mp'=8] {'mp'}, use_global_device_ids=true, to_apply=%region_3.4 | all-reduce | flops 192 | bytes 1536 | tf_op jit(solution)/shard_map/psum | solution.py:215
  41.5 0.8 multiply_convert_fusion
  42.4 5.8 %collective-permute-start = (bf16[192,768]{1,0:T(8,128)(2,1)S(1)}, bf16[192,768]{1,0:T(8,128)(2,1)S(1)}, u32[]{:S(2)}, u32[]{:S(2)}) collective-permute-start(bf16[192,768]{1,0:T(8,128)(2,1)S(1)} %multiply_convert_fusion), channel_id=1, source_target_pairs={{0,0},{1,1},{2,8},{3,9},{4,16},{5,17},{6,24},{7,25},{8,2},{9,3},{1... | collective-permute-start | bytes 884744 | tf_op jit(solution)/shard_map/ppermute | solution.py:225
  48.2 19.7 %collective-permute-done = bf16[192,768]{1,0:T(8,128)(2,1)S(1)} collective-permute-done((bf16[192,768]{1,0:T(8,128)(2,1)S(1)}, bf16[192,768]{1,0:T(8,128)(2,1)S(1)}, u32[]{:S(2)}, u32[]{:S(2)}) %collective-permute-start) | collective-permute-done | bytes 294944 | tf_op jit(solution)/shard_map/ppermute | solution.py:225
  67.9 0.0 copy-start.3
  67.9 0.7 copy-done.3
  68.6 0.0 all-gather.3.cloned.1.call-update
  68.6 0.0 reduce-scatter.2.cloned.1.call-start
  68.7 29.6 %all-gather.3.cloned.1.call-done = bf16[1536,768]{1,0:T(8,128)(2,1)} async-done(((bf16[192,768]{1,0:T(8,128)(2,1)}), bf16[1536,768]{1,0:T(8,128)(2,1)}) %all-gather.3.cloned.1.call-update) | async-done | bytes 2359312 | tf_op jit(solution)/shard_map/all_gather | solution.py:226
  98.2 0.0 copy-start.5
  98.2 4.2 %copy.11 = bf16[4,2,192,768]{3,1,2,0:T(2,128)(2,1)S(1)} copy(bf16[4,2,192,768]{3,2,1,0:T(8,128)(2,1)} %bitcast.19) | data formatting | bytes 4718592 | tf_op jit(solution)/shard_map/reshape | solution.py:228
  102.5 0.0 slice-start
  102.5 0.4 copy.13
  102.9 0.0 copy-done.2
  103.0 0.0 copy-done.5
  103.0 0.0 copy-start.1
  103.0 0.0 slice-start.1
  103.0 0.0 slice-start.2
  103.0 7.7 %convolution_convert_fusion.part = bf16[768,3072]{1,0:T(8,128)(2,1)S(1)} fusion(bf16[768,1536]{1,0:T(8,128)(2,1)S(1)} %bitcast.20, bf16[1536,3072]{1,0:T(8,128)(2,1)S(1)} %copy-done.5), kind=kOutput, calls=%fused_computation | convolution fusion | flops 7250116608 | bytes 16515072 | tf_op jit(solution)/shard_map/dot_general | solution.py:232
  110.7 0.0 copy-done.1
  110.7 120.6 %shard_map.91 = bf16[768,3072]{1,0:T(8,128)(2,1)S(1)} custom-call(bf16[768,3072]{1,0:T(8,128)(2,1)S(1)} %convolution_convert_fusion.part, f32[1,3072]{1,0:T(1,128)S(1)} %bitcast.16), custom_call_target="tpu_custom_call" | custom-call | tf_op jit(solution)/shard_map/pallas_call | solution.py:166
  231.3 0.0 slice-done
  231.3 0.0 slice-done.1
  231.3 0.0 slice-done.2
  231.3 8.8 %convolution_convert_fusion.1 = bf16[768,1536]{1,0:T(8,128)(2,1)} fusion(bf16[768,3072]{1,0:T(8,128)(2,1)S(1)} %shard_map.91, bf16[3072,1536]{1,0:T(8,128)(2,1)S(1)} %bitcast.22), kind=kOutput, calls=%fused_computation.1 | convolution fusion | flops 7248936960 | bytes 16515072 | tf_op jit(solution)/shard_map/dot_general | solution.py:234
  240.1 5.0 %reshape.34 = bf16[4,192,2,768]{3,2,1,0:T(2,128)(2,1)S(1)} reshape(bf16[768,1536]{1,0:T(8,128)(2,1)} %convolution_convert_fusion.1) | data formatting | bytes 4718592 | tf_op jit(solution)/shard_map/reshape | solution.py:238
  245.1 0.0 copy-start.4
  245.1 1.7 copy.12
  246.8 0.0 reduce-scatter.2.cloned.1.call-update
  246.8 42.0 %reduce-scatter.2.cloned.1.call-done = bf16[192,768]{1,0:T(8,128)(2,1)} async-done(((bf16[1536,768]{1,0:T(8,128)(2,1)}), bf16[192,768]{1,0:T(8,128)(2,1)}) %reduce-scatter.2.cloned.1.call-update) | async-done | bytes 294928 | tf_op jit(solution)/shard_map/reduce_scatter | solution.py:242
  288.8 3.4 %collective-permute-start.1 = (bf16[192,768]{1,0:T(8,128)(2,1)}, bf16[192,768]{1,0:T(8,128)(2,1)S(1)}, u32[]{:S(2)}, u32[]{:S(2)}) collective-permute-start(bf16[192,768]{1,0:T(8,128)(2,1)} %reduce-scatter.2.cloned.1.call-done), channel_id=1, source_target_pairs={{0,0},{1,1},{8,2},{9,3},{16,4},{17,5},{24,6},{25,7},{2,8},{3,9},{1... | collective-permute-start | bytes 884744 | tf_op jit(solution)/shard_map/ppermute | solution.py:243
  292.2 20.8 %collective-permute-done.1 = bf16[192,768]{1,0:T(8,128)(2,1)S(1)} collective-permute-done((bf16[192,768]{1,0:T(8,128)(2,1)}, bf16[192,768]{1,0:T(8,128)(2,1)S(1)}, u32[]{:S(2)}, u32[]{:S(2)}) %collective-permute-start.1) | collective-permute-done | bytes 294944 | tf_op jit(solution)/shard_map/ppermute | solution.py:243
  313.0 0.0 copy-done.4
  313.0 1.9 add_add_fusion
  (4 shorter events, 0.0 us)
Async XLA Ops:
  6.5 9.5 %copy-start = (bf16[588,768]{1,0:T(8,128)(2,1)S(1)}, bf16[588,768]{1,0:T(8,128)(2,1)}, u32[]{:S(2)}) copy-start(bf16[588,768]{1,0:T(8,128)(2,1)} %param.10) | copy-start | bytes 2709508
  6.5 91.7 %all-gather.3.cloned.1.call-start = ((), (), s32[]{:S(2)}) async-start(), calls=%async_computation.2 | async-start | bytes 2654208 | tf_op jit(solution)/shard_map/all_gather | solution.py:226
  18.5 84.5 %copy-start.2 = (f32[192,768]{1,0:T(8,128)}, f32[192,768]{1,0:T(8,128)S(1)}, u32[]{:S(2)}) copy-start(f32[192,768]{1,0:T(8,128)S(1)} %get-tuple-element.6) | copy-start | bytes 1769476
  42.4 25.5 %collective-permute-start = (bf16[192,768]{1,0:T(8,128)(2,1)S(1)}, bf16[192,768]{1,0:T(8,128)(2,1)S(1)}, u32[]{:S(2)}, u32[]{:S(2)}) collective-permute-start(bf16[192,768]{1,0:T(8,128)(2,1)S(1)} %multiply_convert_fusion), channel_id=1, source_target_pairs={{0,0},{1,1},{2,8},{3,9},{4,16},{5,17},{6,24},{7,25},{8,2},{9,3},{1... | collective-permute-start | bytes 884744 | tf_op jit(solution)/shard_map/ppermute | solution.py:225
  67.9 0.7 copy-start.3
  68.6 220.1 %reduce-scatter.2.cloned.1.call-start = ((), (), s32[]{:S(2)}) async-start(), calls=%async_computation.1 | async-start | bytes 2654208 | tf_op jit(solution)/shard_map/reduce_scatter | solution.py:242
  98.2 4.7 %copy-start.5 = (bf16[1536,3072]{1,0:T(8,128)(2,1)S(1)}, bf16[1536,3072]{1,0:T(8,128)(2,1)}, u32[]{:S(2)}) copy-start(bf16[1536,3072]{1,0:T(8,128)(2,1)} %param.14) | copy-start | bytes 28311556
  102.5 128.8 %slice-start = ((s8[9437184]{0:T(1024)(128)(4,1)}), s8[4194304]{0:T(1024)(128)(4,1)S(1)}, s32[]{:S(2)}) async-start(s8[9437184]{0:T(1024)(128)(4,1)} %bitcast.21), calls=%async_computation.3 | async-start | bytes 8388608
  103.0 7.7 %copy-start.1 = (f32[3072]{0:T(1024)S(1)}, f32[3072]{0:T(1024)}, u32[]{:S(2)}) copy-start(f32[3072]{0:T(1024)} %param.15) | copy-start | bytes 36868
  103.0 128.3 %slice-start.1 = ((s8[9437184]{0:T(1024)(128)(4,1)}), s8[4194304]{0:T(1024)(128)(4,1)S(1)}, s32[]{:S(2)}) async-start(s8[9437184]{0:T(1024)(128)(4,1)} %bitcast.21), calls=%async_computation.4 | async-start | bytes 8388608
  103.0 128.3 %slice-start.2 = ((s8[9437184]{0:T(1024)(128)(4,1)}), s8[1048576]{0:T(1024)(128)(4,1)S(1)}, s32[]{:S(2)}) async-start(s8[9437184]{0:T(1024)(128)(4,1)} %bitcast.21), calls=%async_computation.5 | async-start | bytes 2097152
  245.1 67.9 %copy-start.4 = (f32[768]{0:T(1024)S(1)}, f32[768]{0:T(1024)}, u32[]{:S(2)}) copy-start(f32[768]{0:T(1024)} %param.17) | copy-start | bytes 9220
  288.8 24.2 %collective-permute-start.1 = (bf16[192,768]{1,0:T(8,128)(2,1)}, bf16[192,768]{1,0:T(8,128)(2,1)S(1)}, u32[]{:S(2)}, u32[]{:S(2)}) collective-permute-start(bf16[192,768]{1,0:T(8,128)(2,1)} %reduce-scatter.2.cloned.1.call-done), channel_id=1, source_target_pairs={{0,0},{1,1},{8,2},{9,3},{16,4},{17,5},{24,6},{25,7},{2,8},{3,9},{1... | collective-permute-start | bytes 884744 | tf_op jit(solution)/shard_map/ppermute | solution.py:243
Sparse Core Ops, SparseCore 0:
  68.7 29.4 all-gather.2
  246.9 41.7 reduce-scatter.1

commit v3 on v2

--- a/solution.py
+++ b/solution.py
@@ -180,6 +180,265 @@
             collective_id=0, has_side_effects=True, vmem_limit_bytes=40 * 1024 * 1024
         ),
     )(part, bias)
+
+PIECES = 4
+MESH = pl.DeviceIdType.MESH
+
+
+def places(n, ratio):
+    i, m = lax.axis_index("dp"), lax.axis_index("mp")
+    parity = lax.rem(m, 2)
+    other = {"mp": m + 1 - 2 * parity}
+    mirror = {"dp": m // ratio, "mp": i * ratio + lax.rem(m, ratio)}
+    alone = jnp.logical_and(m // ratio == i, i * ratio + lax.rem(m, ratio) == m)
+    return m, parity, other, mirror, alone
+
+
+def slot_of(n, ratio, m):
+    return lax.rem(m, ratio) * n + m // ratio
+
+
+def greet(chips, m, parity, other, mirror, alone):
+    barrier = pltpu.get_barrier_semaphore()
+    pl.semaphore_signal(barrier, inc=1, device_id=other, device_id_type=MESH)
+
+    def call(j, carry):
+        mate = 2 * lax.rem(m // 2 + j, chips) + parity
+        pl.semaphore_signal(barrier, inc=1, device_id={"mp": mate}, device_id_type=MESH)
+        return carry
+
+    lax.fori_loop(1, chips, call, 0)
+
+    @pl.when(jnp.logical_not(alone))
+    def _():
+        pl.semaphore_signal(barrier, inc=1, device_id=mirror, device_id_type=MESH)
+        pl.semaphore_wait(barrier, chips + 1)
+
+    @pl.when(alone)
+    def _():
+        pl.semaphore_wait(barrier, chips)
+
+
+def push(src, dst, send_sem, recv_sem, to):
+    return pltpu.make_async_remote_copy(
+        src_ref=src,
+        dst_ref=dst,
+        send_sem=send_sem,
+        recv_sem=recv_sem,
+        device_id=to,
+        device_id_type=MESH,
+    )
+
+
+def gather_kernel(n, ratio, own, out, send_sems, held_sems, block_sems):
+    m, parity, other, mirror, alone = places(n, ratio)
+    members, rows, _ = out.shape
+    chips = members // 2
+    tall = rows // PIECES
+    held = slot_of(n, ratio, m)
+    target = slot_of(n, ratio, mirror["mp"])
+    greet(chips, m, parity, other, mirror, alone)
+
+    def piece(slot, s):
+        return out.at[slot, pl.ds(s * tall, tall)]
+
+    def first(s):
+        return push(
+            own.at[pl.ds(s * tall, tall)], piece(target, s), send_sems.at[0], held_sems.at[s], mirror
+        )
+
+    @pl.when(jnp.logical_not(alone))
+    def _():
+        for s in range(PIECES):
+            first(s).start()
+
+    @pl.when(alone)
+    def _():
+        out[held] = own[...]
+
+    def share(slot, sender, s, to):
+        block = piece(slot, s)
+        return push(block, block, send_sems.at[1], block_sems.at[sender, s], to)
+
+    for s in range(PIECES):
+
+        @pl.when(jnp.logical_not(alone))
+        def _(s=s):
+            push(piece(held, s), piece(held, s), send_sems.at[0], held_sems.at[s], mirror).wait_recv()
+
+        def spread(j, carry, s=s):
+            share(held, m, s, {"mp": 2 * lax.rem(m // 2 + j, chips) + parity}).start()
+            return carry
+
+        lax.fori_loop(1, chips, spread, 0)
+        share(held, m, s, other).start()
+
+    for s in range(PIECES):
+
+        def forward(j, carry, s=s):
+            sender = 2 * lax.rem(m // 2 + j, chips) + parity
+            copy = share(slot_of(n, ratio, sender), sender, s, other)
+            copy.wait_recv()
+            copy.start()
+            return carry
+
+        lax.fori_loop(1, chips, forward, 0)
+
+    for s in range(PIECES):
+
+        def arrive(j, carry, s=s):
+            sender = 2 * lax.rem(m // 2 + j, chips) + 1 - parity
+            share(slot_of(n, ratio, sender), sender, s, other).wait_recv()
+            return carry
+
+        lax.fori_loop(0, chips, arrive, 0)
+
+    @pl.when(jnp.logical_not(alone))
+    def _():
+        push(own, own, send_sems.at[0], held_sems.at[0], mirror).wait_send()
+
+    sent = out.at[pl.ds(0, members - 1)]
+    push(sent, sent, send_sems.at[1], held_sems.at[0], other).wait_send()
+
+
+def blocks_of(n, members, own):
+    vmem = pl.BlockSpec(memory_space=pltpu.VMEM)
+    return pl.pallas_call(
+        functools.partial(gather_kernel, n, members // n),
+        out_shape=jax.ShapeDtypeStruct((members,) + own.shape, jnp.bfloat16),
+        in_specs=[vmem],
+        out_specs=vmem,
+        scratch_shapes=[
+            pltpu.SemaphoreType.DMA((2,)),
+            pltpu.SemaphoreType.DMA((PIECES,)),
+            pltpu.SemaphoreType.DMA((members, PIECES)),
+        ],
+        compiler_params=pltpu.CompilerParams(
+            collective_id=1, has_side_effects=True, vmem_limit_bytes=40 * 1024 * 1024
+        ),
+    )(own)
+
+
+def scatter_kernel(
+    n, ratio, parts, out, pair_in, plane_in, done, send_sems, pair_sems, plane_sems, out_sems
+):
+    m, parity, other, mirror, alone = places(n, ratio)
+    members, rows, _ = parts.shape
+    chips = members // 2
+    tall = rows // PIECES
+    here = m // 2
+    greet(chips, m, parity, other, mirror, alone)
+
+    def lines(s):
+        return pl.ds(s * tall, tall)
+
+    def own_part(chip, side, s):
+        return parts.at[slot_of(n, ratio, 2 * chip + side), lines(s)]
+
+    def to_pair(chip, s):
+        return push(
+            own_part(chip, 1 - parity, s),
+            pair_in.at[chip, lines(s)],
+            send_sems.at[0],
+            pair_sems.at[chip, s],
+            other,
+        )
+
+    def to_plane(chip, s):
+        return push(
+            pair_in.at[chip, lines(s)],
+            plane_in.at[here, lines(s)],
+            send_sems.at[1],
+            plane_sems.at[here, s],
+            {"mp": 2 * chip + parity},
+        )
+
+    def from_plane(chip, s):
+        landed = plane_in.at[chip, lines(s)]
+        return push(landed, landed, send_sems.at[1], plane_sems.at[chip, s], other)
+
+    def home(s):
+        return push(
+            done.at[lines(s)], out.at[lines(s)], send_sems.at[2], out_sems.at[s], mirror
+        )
+
+    def pair_sum(chip, s):
+        to_pair(chip, s).wait_recv()
+        return pair_in[chip, lines(s)].astype(jnp.float32) + own_part(chip, parity, s)[...].astype(
+            jnp.float32
+        )
+
+    for s in range(PIECES):
+
+        def give(j, carry, s=s):
+            to_pair(lax.rem(here + j, chips), s).start()
+            return carry
+
+        lax.fori_loop(1, chips + 1, give, 0)
+
+    for s in range(PIECES):
+
+        def pass_on(j, carry, s=s):
+            chip = lax.rem(here + j, chips)
+            pair_in[chip, lines(s)] = pair_sum(chip, s).astype(jnp.bfloat16)
+            to_plane(chip, s).start()
+            return carry
+
+        lax.fori_loop(1, chips, pass_on, 0)
+
+    for s in range(PIECES):
+
+        def add(j, total, s=s):
+            chip = lax.rem(here + j, chips)
+            from_plane(chip, s).wait_recv()
+            return total + plane_in[chip, lines(s)].astype(jnp.float32)
+
+        total = pair_sum(here, s)
+        for j in range(1, chips):
+            total = add(j, total)
+        done[lines(s)] = total.astype(jnp.bfloat16)
+
+        @pl.when(jnp.logical_not(alone))
+        def _(s=s):
+            home(s).start()
+
+    @pl.when(alone)
+    def _():
+        out[...] = done[...]
+
+    @pl.when(jnp.logical_not(alone))
+    def _():
+        for s in range(PIECES):
+            home(s).wait_recv()
+        push(done, done, send_sems.at[2], out_sems.at[0], mirror).wait_send()
+
+    push(pair_in, pair_in, send_sems.at[0], out_sems.at[0], other).wait_send()
+    passed = plane_in.at[pl.ds(0, chips - 1)]
+    push(passed, passed, send_sems.at[1], out_sems.at[0], other).wait_send()
+
+
+def sum_of(n, parts):
+    members, rows, width = parts.shape
+    chips = members // 2
+    vmem = pl.BlockSpec(memory_space=pltpu.VMEM)
+    return pl.pallas_call(
+        functools.partial(scatter_kernel, n, members // n),
+        out_shape=jax.ShapeDtypeStruct((rows, width), jnp.bfloat16),
+        in_specs=[vmem],
+        out_specs=vmem,
+        scratch_shapes=[
+            pltpu.VMEM((chips, rows, width), jnp.bfloat16),
+            pltpu.VMEM((chips, rows, width), jnp.bfloat16),
+            pltpu.VMEM((rows, width), jnp.bfloat16),
+            pltpu.SemaphoreType.DMA((3,)),
+            pltpu.SemaphoreType.DMA((chips, PIECES)),
+            pltpu.SemaphoreType.DMA((chips, PIECES)),
+            pltpu.SemaphoreType.DMA((PIECES,)),
+        ],
+        compiler_params=pltpu.CompilerParams(
+            collective_id=2, has_side_effects=True, vmem_limit_bytes=40 * 1024 * 1024
+        ),
+    )(parts)
 
 
 def per_device(
@@ -217,30 +476,25 @@
         jnp.bfloat16
     )
 
-    there = []
-    for r in range(n_dp):
-        for c in range(n_mp):
-            there.append((r * n_mp + c, (c // ratio) * n_mp + r * ratio + c % ratio))
-    back = [(b, a) for a, b in there]
-    moved = lax.ppermute(normed, ("dp", "mp"), there)
-    blocks = lax.all_gather(moved, "mp", axis=0, tiled=False)
-    own_rows = (
-        blocks.reshape(n_dp, ratio, group_rows, width)
-        .transpose(0, 2, 1, 3)
-        .reshape(n_dp * group_rows, ratio * width)
-    )
-    preact_part = jnp.dot(own_rows, inner_weight, preferred_element_type=jnp.float32)
+    blocks = blocks_of(n_dp, n_mp, normed).reshape(ratio, n_dp * group_rows, width)
+    preact_part = 0.0
+    for b in range(ratio):
+        preact_part = preact_part + jnp.dot(
+            blocks[b],
+            inner_weight[b * width : (b + 1) * width],
+            preferred_element_type=jnp.float32,
+        )
     all_hidden = hidden_of(n_dp, preact_part.astype(jnp.bfloat16), inner_bias[None, :])
-    partials = jnp.dot(all_hidden, outer_weight, preferred_element_type=jnp.float32).astype(
-        jnp.bfloat16
-    )
-    partials = (
-        partials.reshape(n_dp, group_rows, ratio, width)
-        .transpose(0, 2, 1, 3)
-        .reshape(n_mp * group_rows, width)
-    )
-    summed = lax.psum_scatter(partials, "mp", scatter_dimension=0, tiled=True)
-    mlp_out = lax.ppermute(summed, ("dp", "mp"), back).astype(jnp.float32)
+    partials = [
+        jnp.dot(
+            all_hidden,
+            outer_weight[:, b * width : (b + 1) * width],
+            preferred_element_type=jnp.float32,
+        ).astype(jnp.bfloat16)
+        for b in range(ratio)
+    ]
+    parts = jnp.stack(partials).reshape(n_mp, group_rows, width)
+    mlp_out = sum_of(n_dp, parts).astype(jnp.float32)
     return residual + mlp_out + outer_bias[None, :]
 
 

time: 322 us -> 251 us (0.78)
  waiting for transfers between devices: 112 us -> 0 us
  Pallas kernels: 121 us -> 186 us
  between operations: 13.6 us -> 0.21 us
  local copies, waits for them, and re-layouts: 12.1 us -> 0.22 us
  starting transfers between devices: 9.25 us -> 0 us
  matrix products: 18.9 us -> 27.8 us
    pallas_call x0 -> x2, Pallas kernels: none -> 62.7 us  [the longest x1 32.4 us: blocks_of(): pl.pallas_call(functools.partial(gather_kernel, n, members // n), out_sha...]
    reduce_scatter x1 -> x0, waiting for transfers between devices: 42 us -> none  [per_device(): summed = lax.psum_scatter(partials, 'mp', scatter_dimension=0, tiled=True)]
    ppermute x2 -> x0, waiting for transfers between devices: 40.5 us -> none  [the longest x1 20.8 us: per_device(): mlp_out = lax.ppermute(summed, ('dp', 'mp'), back).astype(jnp.float32)]
    all_gather x1 -> x0, waiting for transfers between devices: 29.6 us -> none  [per_device(): blocks = lax.all_gather(moved, 'mp', axis=0, tiled=False)]
    reshape x3 -> x0, local copies, waits for them, and re-layouts: 10.9 us -> none  [the longest x2 6.68 us: per_device(): partials.reshape(n_dp, group_rows, ratio, width).transpose(0, 2, 1, 3)]
    ppermute x2 -> x0, starting transfers between devices: 9.21 us -> none  [the longest x1 5.83 us: per_device(): moved = lax.ppermute(normed, ('dp', 'mp'), there)]
    dot_general x2 -> x4, matrix products: 16.5 us -> 25.4 us  [the longest x2 15.2 us: per_device(): jnp.dot(blocks[b], inner_weight[b * width:(b + 1) * width], preferred_ele...]
  transfers between devices with their start and end apart: 4 -> 0, of which waited for: 4 -> 0; matrix products, arithmetic and copies ran while one was open for 0% -> 0% of each run, Pallas kernels for 0% -> 0%
where the time goes in v3:
time: 251 us; the launch traced here: 249 us
  Pallas kernels  186 us (74%)
  blocking collectives  32.3 us (13%)
  matrix products  27.8 us (11%)
    pallas_call x1, Pallas kernels, hidden_of(): pl.pallas_call(functools.partial(line_kernel, n), out_shape=jax.ShapeDtyp...  124 us
    pallas_call x1, Pallas kernels, blocks_of(): pl.pallas_call(functools.partial(gather_kernel, n, members // n), out_sha...  32.4 us
    pallas_call x1, Pallas kernels, sum_of(): pl.pallas_call(functools.partial(scatter_kernel, n, members // n), out_sh...  30.3 us
    dot_general x2, matrix products, per_device(): jnp.dot(blocks[b], inner_weight[b * width:(b + 1) * width], preferred_ele...  15.2 us
    psum x1, blocking collectives, per_device(): row_var = lax.psum(jnp.sum(centred * centred, axis=1), 'mp') / model_width  11.8 us
    psum x1, blocking collectives, per_device(): row_total = lax.psum(jnp.sum(residual, axis=1), 'mp')  11 us
    dot_general x2, matrix products, per_device(): jnp.dot(all_hidden, outer_weight[:, b * width:(b + 1) * width], preferred...  10.1 us
    all_gather x1, blocking collectives, per_device(): all_patches = lax.all_gather(patches, 'mp', axis=1, tiled=True)  9.44 us

profile of v3, /device:TPU:2, one launch (start us, length us, event | category | flops | bytes accessed | tf_op | source)
XLA Modules:
  0.0 249.0 jit_solution(17494374328069298876)
XLA Ops:
  0.0 0.0 copy-start
  0.0 9.4 %all_gather.3 = bf16[588,192]{0,1:T(8,128)(2,1)S(1)} all-gather(bf16[588,24]{0,1:T(8,128)(2,1)} %param.9), channel_id=1, replica_groups=mesh['dp'=4,'mp'=8] {'mp'}, dimensions={1}, use_global_device_ids=true | all-gather | bytes 254016 | tf_op jit(solution)/shard_map/all_gather | solution.py:467
  9.5 0.0 copy-done
  9.5 1.1 convolution_add_fusion
  10.6 1.4 fusion.22
  11.9 11.0 %psum.14 = f32[192]{0:T(256)S(1)} all-reduce(f32[192]{0:T(256)S(1)} %get-tuple-element.7), channel_id=1, replica_groups=mesh['dp'=4,'mp'=8] {'mp'}, use_global_device_ids=true, to_apply=%region_1.2 | all-reduce | flops 192 | bytes 1536 | tf_op jit(solution)/shard_map/psum | solution.py:471
  22.9 0.2 multiply_reduce_fusion
  23.1 11.8 %psum.15 = f32[192]{0:T(256)S(1)} all-reduce(f32[192]{0:T(256)S(1)} %multiply_reduce_fusion), channel_id=1, replica_groups=mesh['dp'=4,'mp'=8] {'mp'}, use_global_device_ids=true, to_apply=%region_3.4 | all-reduce | flops 192 | bytes 1536 | tf_op jit(solution)/shard_map/psum | solution.py:474
  35.0 0.8 multiply_convert_fusion.own
  35.8 32.4 %shard_map.91 = bf16[8,192,768]{2,1,0:T(8,128)(2,1)S(1)} custom-call(bf16[192,768]{1,0:T(8,128)(2,1)S(1)} %multiply_convert_fusion.own), custom_call_target="tpu_custom_call" | custom-call | tf_op jit(solution)/shard_map/pallas_call | solution.py:306
  68.3 0.0 slice-start
  68.3 0.2 fusion.21
  68.5 0.0 slice-start.1
  68.5 0.0 slice-start.2
  68.5 8.8 %fusion.5 = f32[768,3072]{1,0:T(8,128)} fusion(bf16[768,768]{1,0:T(8,128)(2,1)S(1)} %bitcast.18, bf16[1536,3072]{1,0:T(8,128)(2,1)} %param.14), kind=kOutput, calls=%fused_computation.6 | convolution fusion | flops 3623878656 | bytes 15335424 | tf_op jit(solution)/shard_map/dot_general | solution.py:482
  77.2 0.0 slice-done
  77.2 0.0 slice-done.1
  77.2 0.0 slice-done.2
  77.3 0.0 copy-start.1
  77.3 6.5 %add_convert_fusion.part = bf16[768,3072]{1,0:T(8,128)(2,1)S(1)} fusion(f32[768,3072]{1,0:T(8,128)} %fusion.5, bf16[768,768]{1,0:T(8,128)(2,1)S(1)} %bitcast.17, bf16[1536,3072]{1,0:T(8,128)(2,1)S(1)} %bitcast.20), kind=kOutput, calls=%fused_computation | convolution fusion | flops 3628597248 | bytes 20054016 | tf_op jit(solution)/shard_map/dot_general | solution.py:482
  83.8 0.0 copy-done.1
  83.8 0.0 slice-start.3
  83.8 123.6 %shard_map.92 = bf16[768,3072]{1,0:T(8,128)(2,1)S(1)} custom-call(bf16[768,3072]{1,0:T(8,128)(2,1)S(1)} %add_convert_fusion.part, f32[1,3072]{1,0:T(1,128)S(1)} %bitcast.16), custom_call_target="tpu_custom_call" | custom-call | tf_op jit(solution)/shard_map/pallas_call | solution.py:166
  207.4 0.0 slice-start.4
  207.4 0.0 slice-start.5
  207.4 6.3 %fusion.13 = bf16[1,768,768]{2,1,0:T(8,128)(2,1)S(1)} fusion(bf16[768,3072]{1,0:T(8,128)(2,1)S(1)} %shard_map.92, bf16[3072,1536]{1,0:T(8,128)(2,1)} %param.16), kind=kOutput, calls=%fused_computation.11 | convolution fusion | flops 3624468480 | bytes 10616832 | tf_op jit(solution)/shard_map/dot_general | solution.py:489
  213.7 0.0 slice-done.3
  213.7 0.0 slice-done.4
  213.7 0.0 slice-done.5
  213.7 3.8 %fusion.16 = bf16[1,768,768]{2,1,0:T(8,128)(2,1)S(1)} fusion(bf16[768,3072]{1,0:T(8,128)(2,1)S(1)} %shard_map.92, bf16[3072,1536]{1,0:T(8,128)(2,1)S(1)} %bitcast.22), kind=kOutput, calls=%fused_computation.12 | convolution fusion | flops 3624468480 | bytes 10616832 | tf_op jit(solution)/shard_map/dot_general | solution.py:489
  217.6 0.0 copy-start.2
  217.6 0.2 pad_maximum_fusion
  217.8 30.3 %shard_map.93 = bf16[192,768]{1,0:T(8,128)(2,1)S(1)} custom-call(bf16[8,192,768]{2,1,0:T(8,128)(2,1)S(1)} %bitcast.15), custom_call_target="tpu_custom_call" | custom-call | tf_op jit(solution)/shard_map/pallas_call | solution.py:424
  248.1 0.0 copy-done.2
  248.1 0.9 add_add_fusion
  (5 shorter events, 0.0 us)
Async XLA Ops:
  0.0 9.5 %copy-start = (bf16[588,768]{1,0:T(8,128)(2,1)S(1)}, bf16[588,768]{1,0:T(8,128)(2,1)}, u32[]{:S(2)}) copy-start(bf16[588,768]{1,0:T(8,128)(2,1)} %param.10) | copy-start | bytes 2709508
  68.3 9.0 %slice-start = ((s8[9437184]{0:T(1024)(128)(4,1)}), s8[4194304]{0:T(1024)(128)(4,1)S(1)}, s32[]{:S(2)}) async-start(s8[9437184]{0:T(1024)(128)(4,1)} %bitcast.19), calls=%async_computation | async-start | bytes 8388608
  68.5 8.8 %slice-start.1 = ((s8[9437184]{0:T(1024)(128)(4,1)}), s8[4194304]{0:T(1024)(128)(4,1)S(1)}, s32[]{:S(2)}) async-start(s8[9437184]{0:T(1024)(128)(4,1)} %bitcast.19), calls=%async_computation.1 | async-start | bytes 8388608
  68.5 8.8 %slice-start.2 = ((s8[9437184]{0:T(1024)(128)(4,1)}), s8[1048576]{0:T(1024)(128)(4,1)S(1)}, s32[]{:S(2)}) async-start(s8[9437184]{0:T(1024)(128)(4,1)} %bitcast.19), calls=%async_computation.2 | async-start | bytes 2097152
  77.3 6.5 %copy-start.1 = (f32[3072]{0:T(1024)S(1)}, f32[3072]{0:T(1024)}, u32[]{:S(2)}) copy-start(f32[3072]{0:T(1024)} %param.15) | copy-start | bytes 36868
  83.8 129.9 %slice-start.3 = ((s8[9437184]{0:T(1024)(128)(4,1)}), s8[4194304]{0:T(1024)(128)(4,1)S(1)}, s32[]{:S(2)}) async-start(s8[9437184]{0:T(1024)(128)(4,1)} %bitcast.21), calls=%async_computation.3 | async-start | bytes 8388608
  207.4 6.3 %slice-start.4 = ((s8[9437184]{0:T(1024)(128)(4,1)}), s8[4194304]{0:T(1024)(128)(4,1)S(1)}, s32[]{:S(2)}) async-start(s8[9437184]{0:T(1024)(128)(4,1)} %bitcast.21), calls=%async_computation.4 | async-start | bytes 8388608
  207.4 6.3 %slice-start.5 = ((s8[9437184]{0:T(1024)(128)(4,1)}), s8[1048576]{0:T(1024)(128)(4,1)S(1)}, s32[]{:S(2)}) async-start(s8[9437184]{0:T(1024)(128)(4,1)} %bitcast.21), calls=%async_computation.5 | async-start | bytes 2097152
  217.6 30.5 %copy-start.2 = (f32[768]{0:T(1024)S(1)}, f32[768]{0:T(1024)}, u32[]{:S(2)}) copy-start(f32[768]{0:T(1024)} %param.17) | copy-start | bytes 9220
